TPU v7x, 16 devices: a whole 2x2x2 slice. The times are simulated.
16 devices in a mesh: dp: 4 (over z, y), tp: 4 (over x, core).
Axes of the slice: x: 2, y: 2, z: 2, core: 2. Of those that a mesh axis runs over, the one named last changes fastest.
Arguments:
- hidden: bfloat16 [4, 2048, 1024], P('dp')
- norm_w: bfloat16 [1024], replicated
- embed_table: bfloat16 [151936, 1024], P('tp')
- labels: int32 [4, 2048], P('dp')
- loss_mask: int32 [4, 2048], P('dp')
Outputs:
- output 1: float32 [], replicated
- output 2: bfloat16 [4, 2048, 1024], P('dp')
- output 3: float32 [1024], replicated
- output 4: float32 [151936, 1024], P('tp')
All inputs are finite; a program needn't handle non-finite values.
Results may differ from a plain program's by a relative error of at most 0.001.
Values sent between devices are 32-bit elements.
A program may use at most 1 GiB of HBM per device.

v0:
```python
import jax
import jax.numpy as jnp
from jax import lax
from jax.sharding import PartitionSpec as P

SOFT_CAP = 30.0


def norm_apply(hid_rows, gain32):
    h32 = hid_rows.astype(jnp.float32)
    inv_rms = lax.rsqrt(jnp.mean(h32 * h32, axis=-1, keepdims=True) + 1e-6)
    return h32 * inv_rms * (1.0 + gain32)


def solution(mesh):
    def local_step(hidden, norm_w, embed_table, labels, loss_mask):
        batch_rows, seq_len, model_dim = hidden.shape
        vocab_local = embed_table.shape[0]
        tokens = batch_rows * seq_len
        hid_rows = hidden.reshape(tokens, model_dim)
        mask_rows = loss_mask.reshape(tokens).astype(jnp.float32)
        tok_count = jnp.maximum(lax.psum(jnp.sum(mask_rows), 'dp'), 1.0)
        normed, norm_back = jax.vjp(norm_apply, hid_rows, norm_w.astype(jnp.float32))
        normed_bf = normed.astype(jnp.bfloat16)
        logits = jnp.einsum('td,vd->tv', normed_bf, embed_table, preferred_element_type=jnp.float32)
        capped = SOFT_CAP * jnp.tanh(logits / SOFT_CAP)
        row_max = lax.pmax(jnp.max(capped, axis=-1), 'tp')
        exp_shift = jnp.exp(capped - row_max[:, None])
        row_sum = lax.psum(jnp.sum(exp_shift, axis=-1), 'tp')
        local_ids = labels.reshape(tokens) - lax.axis_index('tp') * vocab_local
        onehot = lax.broadcasted_iota(jnp.int32, (1, vocab_local), 1) == local_ids[:, None]
        picked = lax.psum(jnp.sum(jnp.where(onehot, capped, 0.0), axis=-1), 'tp')
        tok_loss = jnp.log(row_sum) + row_max - picked
        mean_loss = lax.psum(jnp.sum(mask_rows * tok_loss), 'dp') / tok_count
        tok_scale = mask_rows / tok_count
        cap_ratio = capped / SOFT_CAP
        grad_logit = ((exp_shift / row_sum[:, None] - onehot.astype(jnp.float32)) * tok_scale[:, None] * (1.0 - cap_ratio * cap_ratio)).astype(jnp.bfloat16)
        grad_part = jnp.einsum('tv,vd->td', grad_logit, embed_table, preferred_element_type=jnp.float32)
        grad_x = lax.psum(grad_part, 'tp')
        grad_rows, grad_gain = norm_back(grad_x)
        grad_gain = lax.psum(grad_gain, 'dp')
        table_part = jnp.einsum('tv,td->vd', grad_logit, normed_bf, preferred_element_type=jnp.float32)
        grad_table = lax.psum(table_part, 'dp')
        return mean_loss, grad_rows.reshape(batch_rows, seq_len, model_dim), grad_gain, grad_table

    return jax.shard_map(local_step, mesh=mesh, in_specs=(P('dp', None, None), P(None), P('tp', None), P('dp', None), P('dp', None)), out_specs=(P(), P('dp', None, None), P(None), P('tp', None)), check_vma=False)
```

profile of v0, /device:TPU:0, one launch (start us, length us, event | category | flops | bytes accessed | tf_op | source)
XLA Modules:
  0.0 3525.1 jit_solution(9997675489005906808)
XLA Ops:
  7.2 0.0 all-reduce.5.cloned.1.call-start
  7.2 1.3 convert_reduce_fusion
  8.5 1.3 convert_element_type.31
  9.8 12.3 psum.52
  22.2 0.7 convert_add_fusion
  22.9 3.1 fusion.8
  25.9 0.6 copy-done.2
  26.5 0.6 copy-done
  27.1 4.1 fusion.14.clone.4
  31.3 189.8 %fusion.2 = (f32[2048]{0:T(1024)S(1)}, f32[2048,37984]{0,1:T(8,128)}) fusion(bf16[37984,1024]{1,0:T(8,128)(2,1)} %param.7, bf16[2048,1024]{1,0:T(8,128)(2,1)} %fusion.14.clone.4), kind=kOutput, calls=%fused_computation.7 | convolution fusion | flops 159549816832 | bytes 393158656 | tf_op jit(solution)/shard_map/td,vd->tv/dot_general | solution.py:25
  221.1 16.5 pmax.7
  238.3 116.7 %fusion.1 = (f32[2048]{0:T(1024)S(1)}, f32[2048]{0:T(1024)S(1)}) fusion(f32[2048,37984]{0,1:T(8,128)} %get-tuple-element.15, f32[2048]{0:T(1024)S(1)} %pmax.7, s32[2048]{0:T(1024)S(1)} %bitcast.27), kind=kLoop, calls=%fused_computation.6 | loop fusion | flops 544534528 | bytes 311197696 | tf_op jit(solution)/shard_map/reduce_sum | solution.py:29
  355.0 11.0 all-reduce
  366.0 0.6 broadcast_divide_fusion
  366.6 162.0 %multiply_convert_fusion = bf16[2048,37984]{0,1:T(8,128)(2,1)} fusion(f32[2048,37984]{0,1:T(8,128)} %get-tuple-element.15, f32[2048]{0:T(1024)S(1)} %get-tuple-element.12, f32[2048]{0:T(1024)S(1)} %get-tuple-element.9, s32[2048]{0:T(1024)S(1)} %bitcast.28, f32[2048]{0:T(1024)S(1)} %pmax.7), kind=kLoop, calls=%fused_computation | loop fusion | flops 933494784 | bytes 466780160 | tf_op jit(solution)/shard_map/convert_element_type | solution.py:37
  528.6 176.5 %fusion.16 = f32[2048,1024]{1,0:T(8,128)} fusion(bf16[2048,37984]{0,1:T(8,128)(2,1)} %multiply_convert_fusion, bf16[37984,1024]{1,0:T(8,128)(2,1)} %param.7), kind=kOutput, calls=%fused_computation.31 | convolution fusion | flops 159316443136 | bytes 241762304 | tf_op jit(solution)/shard_map/tv,vd->td/dot_general | solution.py:38
  705.1 0.0 all-reduce.7.cloned.1.call-start
  705.2 176.1 %fusion.11 = f32[37984,1024]{1,0:T(8,128)} fusion(bf16[2048,37984]{0,1:T(8,128)(2,1)} %multiply_convert_fusion, bf16[1,2048,1024]{2,1,0:T(8,128)(2,1)} %param.5, f32[1024]{0:T(1024)S(1)} %copy-done.5, f32[2048]{0:T(1024)S(1)} %copy-done.1), kind=kOutput, calls=%fused_computation.21 | convolution fusion | flops 159324831744 | bytes 315371520 | tf_op jit(solution)/shard_map/tv,td->vd/dot_general | solution.py:42
  881.3 0.0 all-reduce.5.cloned.1.call-done
  881.3 6.1 fusion.6
  887.4 9.3 all-reduce.1
  897.3 6.9 fusion.10
  904.3 2510.5 %all-reduce.7.cloned.1.call-done = f32[37984,1024]{1,0:T(8,128)} async-done(((f32[37984,1024]{1,0:T(8,128)}), f32[37984,1024]{1,0:T(8,128)}) %all-reduce.7.cloned.1.call-update) | async-done | bytes 155582480 | tf_op jit(solution)/shard_map/psum | solution.py:43
  3414.7 102.0 %copy.11 = f32[37984,1024]{1,0:T(8,128)} copy(f32[37984,1024]{1,0:T(8,128)} %all-reduce.7.cloned.1.call-done) | data formatting | bytes 311164928
  (19 shorter events, 0.1 us)
Async XLA Ops:
  7.2 874.2 %all-reduce.5.cloned.1.call-start = ((), (), s32[]{:S(2)}) async-start(), calls=%async_computation | async-start | bytes 16777216 | tf_op jit(solution)/shard_map/psum | solution.py:39
  22.9 3.7 copy-start.4
  25.9 0.6 copy-start.2
  26.5 0.6 copy-start
  31.3 207.0 %copy-start.7 = (s32[1,2048]{1,0:T(1,128)S(1)}, s32[1,2048]{1,0:T(1,128)}, u32[]{:S(2)}) copy-start(s32[1,2048]{1,0:T(1,128)} %param.8) | copy-start | bytes 24580
  238.3 127.7 %copy-start.6 = (f32[1,2048]{1,0:T(1,128)S(1)}, f32[1,2048]{1,0:T(1,128)}, u32[]{:S(2)}) copy-start(f32[1,2048]{1,0:T(1,128)} %convert_element_type.31) | copy-start | bytes 24580
  528.6 176.6 %copy-start.1 = (f32[2048]{0:T(1024)S(1)}, f32[2048]{0:T(1024)}, u32[]{:S(2)}) copy-start(f32[2048]{0:T(1024)} %copy-done) | copy-start | bytes 24580
  528.6 176.6 %copy-start.5 = (f32[1024]{0:T(1024)S(1)}, f32[1024]{0:T(1024)}, u32[]{:S(2)}) copy-start(f32[1024]{0:T(1024)} %copy-done.4) | copy-start | bytes 12292
  705.1 2709.6 %all-reduce.7.cloned.1.call-start = ((), (), s32[]{:S(2)}) async-start(), calls=%async_computation.1 | async-start | bytes 311164928 | tf_op jit(solution)/shard_map/psum | solution.py:43
  881.3 16.0 copy-start.3
Sparse Core Ops, SparseCore 0:
  705.3 147.4 all-reduce.4
  881.4 2533.2 all-reduce.6
where the time goes:
time: 3530 us
  waiting for transfers between devices  2510 us (71%)
  matrix products  542 us (15%)
  other arithmetic  303 us (9%)
  local copies, waits for them, and re-layouts  103 us (3%)
  blocking collectives  49.1 us (1%)
    psum x1, waiting for transfers between devices, local_step(): grad_table = lax.psum(table_part, 'dp')  2510 us
    dot_general x1, matrix products, local_step(): jnp.einsum('td,vd->tv', normed_bf, embed_table, preferred_element_type=jn...  190 us
    dot_general x1, matrix products, local_step(): jnp.einsum('tv,vd->td', grad_logit, embed_table, preferred_element_type=j...  177 us
    dot_general x1, matrix products, local_step(): jnp.einsum('tv,td->vd', grad_logit, normed_bf, preferred_element_type=jnp...  176 us
    convert_element_type x1, other arithmetic, local_step(): ((exp_shift / row_sum[:, None] - onehot.astype(jnp.float32)) * tok_scale[...  162 us
    reduce_sum x1, other arithmetic, local_step(): row_sum = lax.psum(jnp.sum(exp_shift, axis=-1), 'tp')  117 us
    unnamed x17, local copies, waits for them, and re-layouts  103 us
  transfers between devices with their start and end apart: 2, of which 1 were waited for; matrix products, arithmetic and copies ran while one was open for 5% of the time, Pallas kernels for 0%

commit v1 on v0

v1 whole, which is shorter than its diff:
```python
import functools
import math

import jax
import jax.numpy as jnp
from jax import lax
from jax.experimental import pallas as pl
from jax.experimental.pallas import tpu as pltpu
from jax.sharding import PartitionSpec as P

SOFT_CAP = 30.0
EXP2_CAP = 30.0 * math.log2(math.e)
VMEM_LIMIT = 67_000_000

CFG = dict(
    VB=1024,
    TS=512,
    RU=624,
    CHUNKS=(1, 3, 3, 2, 1),
    RD=592,
    CALLS=(6, 6, 6, 4),
    ABSORB=((0, 1), (), (2,), (3,)),
)
ANY = pl.BlockSpec(memory_space=pl.ANY)


def params(**kw):
    return pltpu.CompilerParams(vmem_limit_bytes=VMEM_LIMIT, **kw)


def dot_nt(a, b):
    return lax.dot_general(a, b, (((1,), (1,)), ((), ())), preferred_element_type=jnp.float32)


def first_pass(x, labels_rel, table):
    tokens, dim = x.shape
    rows = table.shape[0]
    vb, ts = CFG["VB"], CFG["TS"]
    n = pl.cdiv(rows, vb)
    last = rows - vb
    parts = tokens // ts

    def kernel(x_ref, lab_ref, e_ref, q_main, q_tail, z_sum, t_lab, z0, z1, carry, lab_b):
        s = pl.program_id(0)

        @pl.when(s == 0)
        def _():
            z_sum[...] = jnp.zeros_like(z_sum)
            t_lab[...] = jnp.zeros_like(t_lab)
            carry[...] = jnp.zeros_like(carry)
            lab_b[...] = jnp.broadcast_to(lab_ref[...], lab_b.shape)

        def elem(k, buf, blk, q_ref, q_row):
            start = jnp.minimum(blk * vb, last)
            ids = lax.broadcasted_iota(jnp.int32, (1, vb), 1) + start
            valid = jnp.logical_and(ids >= blk * vb, blk >= 0)
            bias = jnp.where(valid, 0.0, -1e30)
            ids = jnp.where(valid, ids, -1)
            for r in range(ts // 8):
                src = slice(r * 8, r * 8 + 8)
                row = slice(k * ts + r * 8, k * ts + r * 8 + 8)
                t = jnp.tanh(buf[src, :] * (1.0 / SOFT_CAP))
                e = jnp.exp2(t * EXP2_CAP + bias)
                q_ref[0, q_row + r * 8 : q_row + r * 8 + 8, :] = e * (1.0 - t * t)
                lab = lab_b[row, :]
                zs, tl = z_sum[row, :], t_lab[row, :]
                for c in range(vb // 128):
                    cs = slice(c * 128, (c + 1) * 128)
                    zs += e[:, cs]
                    tl += jnp.where(ids[:, cs] == lab, t[:, cs], 0.0)
                z_sum[row, :] = zs
                t_lab[row, :] = tl

        def dot(k, buf):
            buf[...] = dot_nt(x_ref[k * ts : (k + 1) * ts, :], e_ref[...])

        def tail():
            elem(parts - 1, carry, s - 1, q_tail, 0)

        @pl.when(s < n)
        def _():
            bufs = [(z0, z1)[k % 2] for k in range(parts - 1)] + [carry]
            dot(0, bufs[0])
            tail()
            for k in range(1, parts):
                dot(k, bufs[k])
                elem(k - 1, bufs[k - 1], s, q_main, (k - 1) * ts)

        @pl.when(s == n)
        def _():
            tail()

    col = pl.BlockSpec((tokens, 128), lambda s: (0, 0))
    return pl.pallas_call(
        kernel,
        grid=(n + 1,),
        in_specs=[
            pl.BlockSpec((tokens, dim), lambda s: (0, 0), pipeline_mode=pl.Buffered(1)),
            pl.BlockSpec((tokens, 1), lambda s: (0, 0), pipeline_mode=pl.Buffered(1)),
            pl.BlockSpec((pl.Element(vb), pl.Element(dim)), lambda s: (jnp.minimum(s * (vb // 16), last // 16) * 16, 0)),
        ],
        out_specs=[
            pl.BlockSpec((1, tokens - ts, vb), lambda s: (jnp.minimum(s, n - 1), 0, 0)),
            pl.BlockSpec((1, ts, vb), lambda s: (jnp.maximum(s - 1, 0), 0, 0)),
            col,
            col,
        ],
        out_shape=[
            jax.ShapeDtypeStruct((n, tokens - ts, vb), jnp.float32),
            jax.ShapeDtypeStruct((n, ts, vb), jnp.float32),
            jax.ShapeDtypeStruct((tokens, 128), jnp.float32),
            jax.ShapeDtypeStruct((tokens, 128), jnp.float32),
        ],
        scratch_shapes=[pltpu.VMEM((ts, vb), jnp.float32)] * 3 + [pltpu.VMEM((tokens, 128), jnp.int32)],
        compiler_params=params(dimension_semantics=("arbitrary",)),
        cost_estimate=pl.CostEstimate(flops=2 * tokens * rows * dim, bytes_accessed=tokens * rows * 4, transcendentals=0),
        name="first_pass",
    )(x, labels_rel, table)


def grad_x(q_main, q_tail, table, a_col, b_col, labels_rel, dep):
    n, ts, vb = q_tail.shape
    tokens = q_main.shape[1] + ts
    rows, dim = table.shape
    last = rows - vb

    def kernel(qm_ref, qt_ref, e_ref, a_ref, b_ref, lab_ref, dep_ref, gx_ref, a_b, b_b, lab_b, *g_bufs):
        s = pl.program_id(0)

        @pl.when(s == 0)
        def _():
            gx_ref[...] = jnp.zeros_like(gx_ref)
            a_b[...] = jnp.broadcast_to(a_ref[...], a_b.shape)
            b_b[...] = jnp.broadcast_to(b_ref[...], b_b.shape)
            lab_b[...] = jnp.broadcast_to(lab_ref[...], lab_b.shape)

        start = jnp.minimum(s * vb, last)
        ids = lax.broadcasted_iota(jnp.int32, (1, vb), 1) + start
        ids = jnp.where(ids >= s * vb, ids, -1)
        for k in range(tokens // ts):
            g_buf = g_bufs[k % 2]
            q_ref, row = (qm_ref, k * ts) if k < tokens // ts - 1 else (qt_ref, 0)
            for r in range(ts // 16):
                sl = slice(k * ts + r * 16, k * ts + r * 16 + 16)
                a, b, lab = a_b[sl, :], b_b[sl, :], lab_b[sl, :]
                for c in range(vb // 128):
                    cs = slice(c * 128, (c + 1) * 128)
                    g = q_ref[0, row + r * 16 : row + r * 16 + 16, cs] * a - jnp.where(ids[:, cs] == lab, b, 0.0)
                    g_buf[r * 16 : r * 16 + 16, cs] = g.astype(jnp.bfloat16)
            gx_ref[k * ts : (k + 1) * ts, :] += jnp.dot(g_buf[...], e_ref[...], preferred_element_type=jnp.float32)

    col = pl.BlockSpec((tokens, 1), lambda s: (0, 0), pipeline_mode=pl.Buffered(1))
    return pl.pallas_call(
        kernel,
        grid=(n,),
        in_specs=[
            pl.BlockSpec((1, tokens - ts, vb), lambda s: (s, 0, 0)),
            pl.BlockSpec((1, ts, vb), lambda s: (s, 0, 0)),
            pl.BlockSpec((pl.Element(vb), pl.Element(dim)), lambda s: (jnp.minimum(s * (vb // 16), last // 16) * 16, 0)),
            col,
            col,
            col,
            ANY,
        ],
        out_specs=pl.BlockSpec((tokens, dim), lambda s: (0, 0)),
        out_shape=jax.ShapeDtypeStruct((tokens, dim), jnp.float32),
        scratch_shapes=[
            pltpu.VMEM((tokens, 128), jnp.float32),
            pltpu.VMEM((tokens, 128), jnp.float32),
            pltpu.VMEM((tokens, 128), jnp.int32),
            pltpu.VMEM((ts, vb), jnp.bfloat16),
            pltpu.VMEM((ts, vb), jnp.bfloat16),
        ],
        compiler_params=params(dimension_semantics=("arbitrary",)),
        cost_estimate=pl.CostEstimate(flops=2 * tokens * rows * dim, bytes_accessed=tokens * rows * 4, transcendentals=0),
        name="grad_x",
    )(q_main, q_tail, table, a_col, b_col, labels_rel, dep)


def table_rows(offset, table, x_all, lab, inv_z, scale, rb, nblk, dep, out=None, out_base=0, out_rows=None, sources=()):
    dim = table.shape[1]
    ntc, _, ts = lab.shape
    tokens = ntc * ts
    in_half = ntc // 2
    pieces = []
    for k, (src, row) in enumerate(sources):
        m = CFG["RU"]
        pieces += [(k, p * m, row + p * m) for p in range(src.shape[0] // m)]
    per_block = ntc // 2 - 1
    assert not pieces or len(pieces) + 2 <= nblk * per_block
    rows_total = out.shape[0] if out is not None else out_rows

    def kernel(off_ref, e_hbm, x_a, x_b, lab_ref, iz_ref, sc_ref, dep_ref, *rest):
        rest, x_hbm = list(rest), (x_a, x_b)
        srcs = [rest.pop(0) for _ in sources]
        if out is not None:
            rest.pop(0)
        o_hbm = rest.pop(0)
        xv, ebuf, z0, z1, g0, g1, acc, xsem, esem, osem = rest[:10]
        if pieces:
            pbuf, lsem, ssem = rest[10:]
        zs, gs = (z0, z1), (g0, g1)
        i = pl.program_id(0)
        slot = lax.rem(i, 2)
        off = off_ref[0]

        def x_copy(j):
            src = x_hbm[j // in_half] if isinstance(j, int) else x_hbm[0]
            row = j % in_half if isinstance(j, int) else 0
            dst = pl.ds(pl.multiple_of(j * ts, ts), ts)
            return pltpu.make_async_copy(src.at[pl.ds(row * ts, ts), :], xv.at[dst, :], xsem.at[j])

        def e_copy(b, sl):
            return pltpu.make_async_copy(e_hbm.at[pl.ds(pl.multiple_of(off + b * rb, 16), rb), :], ebuf.at[sl], esem.at[sl])

        def o_copy(b, sl):
            return pltpu.make_async_copy(acc.at[sl], o_hbm.at[pl.ds(pl.multiple_of(out_base + b * rb, 8), rb), :], osem.at[sl])

        @pl.when(i == 0)
        def _():
            e_copy(0, 0).start()
            for j in range(ntc):
                x_copy(j).start()

        @pl.when(i + 1 < nblk)
        def _():
            e_copy(i + 1, 1 - slot).start()

        e_copy(i, slot).wait()

        @pl.when(i >= 2)
        def _():
            o_copy(i - 2, slot).wait()

        def wait_x(*js):
            @pl.when(i == 0)
            def _():
                for j in js:
                    x_copy(j).wait()

        def xs(j):
            return xv[pl.ds(pl.multiple_of(j * ts, ts), ts), :]

        def dot1(j, p):
            zs[p][...] = dot_nt(ebuf[slot], xs(j))

        def elem(j, p):
            rel = lab_ref[j] - (off + i * rb)
            iz, sc = iz_ref[j], sc_ref[j]
            for r in range(rb // 16):
                sl = slice(r * 16, r * 16 + 16)
                t = jnp.tanh(zs[p][sl, :] * (1.0 / SOFT_CAP))
                e = jnp.exp2(t * EXP2_CAP) * iz
                ids = lax.broadcasted_iota(jnp.int32, (16, ts), 0) + r * 16
                d = jnp.where(ids == rel, e - 1.0, e)
                gs[p][sl, :] = (d * sc * (1.0 - t * t)).astype(jnp.bfloat16)

        def dot2(j, p):
            acc[slot] += jnp.dot(gs[p][...], xs(j), preferred_element_type=jnp.float32)

        def piece_step(it):
            if not pieces:
                return
            for idx, (k, a, b) in enumerate(pieces):
                m = CFG["RU"]
                load = pltpu.make_async_copy(srcs[k].at[a : a + m, :], pbuf.at[idx % 2], lsem.at[idx % 2])
                store = pltpu.make_async_copy(pbuf.at[idx % 2], o_hbm.at[b : b + m, :], ssem.at[idx % 2])

                @pl.when(it == idx)
                def _():
                    if idx >= 2:
                        pltpu.make_async_copy(pbuf.at[idx % 2], o_hbm.at[0:m, :], ssem.at[idx % 2]).wait()
                    load.start()

                @pl.when(it == idx + 1)
                def _():
                    load.wait()
                    store.start()

        acc[slot] = jnp.zeros(acc.shape[1:], acc.dtype)
        wait_x(0, 1)
        dot1(0, 0)
        elem(0, 0)
        dot1(1, 1)

        def body(jj, c):
            j = 2 * jj
            wait_x(j, j + 1)
            piece_step(i * per_block + jj - 1)
            dot2(j - 2, 0)
            elem(j - 1, 1)
            dot1(j, 0)
            dot2(j - 1, 1)
            elem(j, 0)
            dot1(j + 1, 1)
            return c

        lax.fori_loop(1, ntc // 2, body, 0)
        dot2(ntc - 2, 0)
        elem(ntc - 1, 1)
        dot2(ntc - 1, 1)
        o_copy(i, slot).start()

        @pl.when(i == nblk - 1)
        def _():
            o_copy(i, slot).wait()
            if nblk >= 2:
                o_copy(i - 1, 1 - slot).wait()
            if pieces:
                for idx in range(max(0, len(pieces) - 2), len(pieces)):
                    m = CFG["RU"]
                    pltpu.make_async_copy(pbuf.at[idx % 2], o_hbm.at[0:m, :], ssem.at[idx % 2]).wait()

    vec = pl.BlockSpec((ntc, 1, ts), lambda i: (0, 0, 0), pipeline_mode=pl.Buffered(1))
    scratch = [
        pltpu.VMEM((tokens, dim), jnp.bfloat16),
        pltpu.VMEM((2, rb, dim), jnp.bfloat16),
        pltpu.VMEM((rb, ts), jnp.float32),
        pltpu.VMEM((rb, ts), jnp.float32),
        pltpu.VMEM((rb, ts), jnp.bfloat16),
        pltpu.VMEM((rb, ts), jnp.bfloat16),
        pltpu.VMEM((2, rb, dim), jnp.float32),
        pltpu.SemaphoreType.DMA((ntc,)),
        pltpu.SemaphoreType.DMA((2,)),
        pltpu.SemaphoreType.DMA((2,)),
    ]
    if pieces:
        scratch += [pltpu.VMEM((2, CFG["RU"], dim), jnp.float32), pltpu.SemaphoreType.DMA((2,)), pltpu.SemaphoreType.DMA((2,))]
    args = [offset, table, *x_all, lab, inv_z, scale, dep] + [s for s, _ in sources] + ([out] if out is not None else [])
    return pl.pallas_call(
        kernel,
        grid=(nblk,),
        in_specs=[pl.BlockSpec(memory_space=pltpu.SMEM), ANY, ANY, ANY, vec, vec, vec, ANY] + [ANY] * (len(args) - 8),
        out_specs=ANY,
        out_shape=jax.ShapeDtypeStruct((rows_total, dim), jnp.float32),
        scratch_shapes=scratch,
        input_output_aliases={len(args) - 1: 0} if out is not None else {},
        compiler_params=params(dimension_semantics=("arbitrary",)),
        cost_estimate=pl.CostEstimate(flops=4 * tokens * rb * nblk * dim, bytes_accessed=tokens * dim * 2, transcendentals=0),
        name="table_rows",
    )(*args)


def place(out, src, row):
    rows, dim = src.shape
    m = rows // 4

    def kernel(src_ref, o_in, o_ref, buf, lsem, ssem):
        loads = [pltpu.make_async_copy(src_ref.at[k * m : (k + 1) * m, :], buf.at[k], lsem.at[k]) for k in range(4)]
        stores = [pltpu.make_async_copy(buf.at[k], o_ref.at[row + k * m : row + (k + 1) * m, :], ssem.at[k]) for k in range(4)]
        for c in loads:
            c.start()
        for a, b in zip(loads, stores):
            a.wait()
            b.start()
        for c in stores:
            c.wait()

    return pl.pallas_call(
        kernel,
        in_specs=[ANY, ANY],
        out_specs=ANY,
        out_shape=jax.ShapeDtypeStruct(out.shape, out.dtype),
        scratch_shapes=[pltpu.VMEM((4, m, dim), jnp.float32), pltpu.SemaphoreType.DMA((4,)), pltpu.SemaphoreType.DMA((4,))],
        input_output_aliases={1: 0},
        compiler_params=params(),
        cost_estimate=pl.CostEstimate(flops=rows * dim, bytes_accessed=rows * dim * 8, transcendentals=0),
        name="place",
    )(src, out)


def norm_apply(hid_rows, gain32):
    h32 = hid_rows.astype(jnp.float32)
    inv_rms = lax.rsqrt(jnp.mean(h32 * h32, axis=-1, keepdims=True) + 1e-6)
    return h32 * inv_rms * (1.0 + gain32)


def solution(mesh):
    n_dp, n_tp = mesh.shape["dp"], mesh.shape["tp"]
    sib = [(i, i ^ 1) for i in range(n_tp)]
    across = [(i, i ^ 2) for i in range(n_tp)]

    def local_step(hidden, norm_w, table, labels, loss_mask):
        batch, seq, dim = hidden.shape
        rows = table.shape[0]
        tokens = batch * seq
        half = tokens // 2
        ts = CFG["TS"]
        dp, tp = lax.axis_index("dp"), lax.axis_index("tp")
        core = lax.rem(tp, 2)
        hid = hidden.reshape(tokens, dim)
        normed, norm_back = jax.vjp(norm_apply, hid, norm_w.astype(jnp.float32))
        x = normed.astype(jnp.bfloat16)
        lab_own = labels.reshape(tokens)
        lab_rel = (lab_own - tp * rows)[:, None]

        def mine(v):
            return jnp.where(core == 0, v[:half], v[half:])

        hid32 = hid.astype(jnp.float32)
        pre = mine(hid32 * lax.rsqrt(jnp.mean(hid32 * hid32, axis=-1, keepdims=True) + 1e-6))
        got = lax.all_gather(pre, "dp", axis=0, tiled=True)

        q_main, q_tail, z_sum, t_lab = first_pass(x, lab_rel, table)
        got, z_sum = lax.optimization_barrier((got, z_sum))
        other = lax.ppermute(got, "tp", sib)
        gain = 1.0 + norm_w.astype(jnp.float32)
        x_all = tuple((v * gain).astype(jnp.bfloat16) for v in (got, other))
        side = jnp.stack([lab_own, loss_mask.reshape(tokens)]).astype(jnp.float32)
        stats = jnp.stack([jnp.sum(z_sum, axis=-1), jnp.sum(t_lab, axis=-1)])
        stats = jnp.concatenate([stats, jnp.where(tp == 0, side, 0.0)])
        stats = lax.dynamic_update_slice(jnp.zeros((n_dp, 4, tokens), jnp.float32), stats[None], (dp, 0, 0))
        stats = lax.psum(stats, ("dp", "tp"))

        split = stats.reshape(n_dp, 4, 2, half)
        split = jnp.where(core == 0, split, split[:, :, ::-1])
        z_all, t_all, lab_all, mask_all = split.transpose(1, 2, 0, 3).reshape(4, -1)
        lab_all = lab_all.astype(jnp.int32)
        count = jnp.maximum(jnp.sum(mask_all), 1.0)
        loss = jnp.sum(mask_all * (jnp.log(z_all) - SOFT_CAP * t_all)) / count
        scale_all = mask_all / count
        shape3 = (n_dp * tokens // ts, 1, ts)
        vecs = ((lab_all - tp * rows).reshape(shape3), (1.0 / z_all).reshape(shape3), scale_all.reshape(shape3))

        own = lax.dynamic_index_in_dim(stats, dp, 0, keepdims=False)
        scale_own = loss_mask.reshape(tokens).astype(jnp.float32) / count
        a_col = (scale_own / own[0])[:, None]
        b_col = (scale_own * (1.0 - own[1] * own[1]))[:, None]

        ru, rd = CFG["RU"], CFG["RD"]
        dep, row, gathered = x, 0, []
        for nblk in CFG["CHUNKS"]:
            off = (row + dp * (nblk * ru)).astype(jnp.int32).reshape(1)
            dep = table_rows(off, table, x_all, *vecs, ru, nblk, dep, out_rows=nblk * ru)
            gathered.append((lax.all_gather(dep, "dp", axis=0, tiled=True), row))
            row += n_dp * nblk * ru

        gx = grad_x(q_main, q_tail, table, a_col, b_col, lab_rel, dep)
        keep = jnp.where(core == 0, gx[:half], gx[half:])
        send = jnp.where(core == 0, gx[half:], gx[:half])
        out = None
        for k, (nblk, absorb) in enumerate(zip(CFG["CALLS"], CFG["ABSORB"])):
            off = jnp.full((1,), row, jnp.int32)
            src = tuple(gathered[c] for c in absorb)
            if k < 3:
                recv = lax.ppermute(send, "tp", (sib, across, sib)[k])
            out = table_rows(off, table, x_all, *vecs, rd, nblk, send, out=out, out_base=row, out_rows=rows, sources=src)
            row += nblk * rd
            if k < 3:
                recv, out = lax.optimization_barrier((recv, out))
            if k < 2:
                send = keep = keep + recv
        gx_all = jnp.where(core == 0, jnp.concatenate([keep, recv]), jnp.concatenate([recv, keep]))
        grad_rows, grad_gain = norm_back(gx_all)
        grad_gain = lax.psum(grad_gain, "dp")
        assert row == rows
        out = place(out, *gathered[-1])
        return loss, grad_rows.reshape(batch, seq, dim), grad_gain, out

    return jax.shard_map(
        local_step,
        mesh=mesh,
        in_specs=(P("dp", None, None), P(None), P("tp", None), P("dp", None), P("dp", None)),
        out_specs=(P(), P("dp", None, None), P(None), P("tp", None)),
        check_vma=False,
    )
```

time: 3530 us -> 1680 us (0.48)
  waiting for transfers between devices: 2510 us -> 67.1 us
  Pallas kernels: 0 us -> 1490 us
  matrix products: 542 us -> 0 us
  other arithmetic: 303 us -> 78.1 us
  local copies, waits for them, and re-layouts: 103 us -> 7.21 us
  blocking collectives: 49.1 us -> 8.97 us
    psum x2 -> x1, waiting for transfers between devices: 2510 us -> 66.9 us  [local_step(): stats = lax.psum(stats, ('dp', 'tp'))]
    pallas_call x0 -> x12, Pallas kernels: none -> 1490 us  [the longest x9 985 us: table_rows(): pl.pallas_call(kernel, grid=(nblk,), in_specs=[pl.BlockSpec(memory_space=...]
    dot_general x3 -> x0, matrix products: 542 us -> none  [the longest x1 190 us: local_step(): jnp.einsum('td,vd->tv', normed_bf, embed_table, preferred_element_type=jn...]
    convert_element_type x2 -> x3, other arithmetic: 163 us -> 28.6 us  [the longest x1 18.4 us: local_step(): x_all = tuple(((v * gain).astype(jnp.bfloat16) for v in (got, other)))]
    reduce_sum x3 -> x4, other arithmetic: 121 us -> 6.86 us  [the longest x2 3.13 us: local_step(): stats = jnp.stack([jnp.sum(z_sum, axis=-1), jnp.sum(t_lab, axis=-1)])]
    unnamed x17 -> x24, local copies, waits for them, and re-layouts: 103 us -> 0.69 us
  transfers between devices with their start and end apart: 2 -> 11, of which waited for: 1 -> 1; matrix products, arithmetic and copies ran while one was open for 5% -> 3% of each run, Pallas kernels for 0% -> 86%
where the time goes in v1:
time: 1680 us; the launch traced here: 1670 us
  Pallas kernels  1490 us (89%)
  other arithmetic  78.1 us (5%)
  waiting for transfers between devices  67.1 us (4%)
  between operations  17.4 us (1%)
    pallas_call x9, Pallas kernels, table_rows(): pl.pallas_call(kernel, grid=(nblk,), in_specs=[pl.BlockSpec(memory_space=...  985 us
    pallas_call x1, Pallas kernels, first_pass(): pl.pallas_call(kernel, grid=(n + 1,), in_specs=[pl.BlockSpec((tokens, dim...  269 us
    pallas_call x1, Pallas kernels, grad_x(): pl.pallas_call(kernel, grid=(n,), in_specs=[pl.BlockSpec((1, tokens - ts,...  224 us
    psum x1, waiting for transfers between devices, local_step(): stats = lax.psum(stats, ('dp', 'tp'))  66.9 us
  transfers between devices with their start and end apart: 11, of which 1 were waited for; matrix products, arithmetic and copies ran while one was open for 3% of the time, Pallas kernels for 86%

profile of v1, /device:TPU:0, one launch (start us, length us, event | category | flops | bytes accessed | tf_op | source)
XLA Modules:
  0.0 1666.7 jit_solution(5504493258427186903)
XLA Ops:
  7.2 3.1 fusion.3
  11.0 4.2 fusion.1
  15.2 3.0 slice_select_fusion
  19.6 269.0 %first_pass.1 = (f32[38,1536,1024]{2,1,0:T(8,128)}, f32[38,512,1024]{2,1,0:T(8,128)}, f32[2048,128]{1,0:T(8,128)}, f32[2048,128]{1,0:T(8,128)}) custom-call(bf16[2048,1024]{1,0:T(8,128)(2,1)} %get-tuple-element.33.x_ref.dep_ref, s32[2048,1]{1,0:T(8,128)} %copy.22.lab_ref, bf16[37984,1024]{1,0:T(8,128)(2,1)} %e_hbm.17), custom_call_target="tpu_custom_call" | custom-call | flops 159316443136 | bytes 311164928 | tf_op jit(solution)/shard_map/first_pass/pallas_call | solution.py:94
  291.0 1.6 reduce_sum.63
  293.9 66.9 %all-reduce.2.cloned.1.call-done = f32[4,4,2048]{2,1,0:T(4,128)} async-done(((f32[4,4,2048]{2,1,0:T(4,128)}), f32[4,4,2048]{2,1,0:T(4,128)}) %all-reduce.2.cloned.1.call-update) | async-done | bytes 131088 | tf_op jit(solution)/shard_map/psum | solution.py:413
  365.2 18.4 %multiply_convert_fusion = (bf16[4096,1024]{1,0:T(8,128)(2,1)}, bf16[4096,1024]{1,0:T(8,128)(2,1)}) fusion(f32[4096,1024]{1,0:T(8,128)} %collective-permute-done, f32[1024]{0:T(1024)S(1)} %copy-done.4, f32[4096,1024]{1,0:T(8,128)} %all-gather.7.cloned.1.call-done), kind=kLoop, calls=%fused_computation | loop fusion | flops 16777216 | bytes 50335744 | tf_op jit(solution)/shard_map/convert_element_type | solution.py:408
  383.6 37.7 %table_rows.9.dep_ref = f32[624,1024]{1,0:T(8,128)} custom-call(s32[1]{0:T(128)} %bitcast.13.off_ref, bf16[37984,1024]{1,0:T(8,128)(2,1)} %e_hbm.17, bf16[4096,1024]{1,0:T(8,128)(2,1)} %get-tuple-element.37.x_a, bf16[4096,1024]{1,0:T(8,128)(2,1)} %get-tuple-element.36.x_b, s32[16,1,512]{2,1,0:T(1,128)} %sub.61.lab_ref, f32[16,1,512]{2,1,0:T(1,128)} %div.81.iz_ref, ...), custom_call_target="tpu_custom_call" | custom-call | flops 20937965568 | bytes 16777216 | tf_op jit(solution)/shard_map/table_rows/pallas_call | solution.py:330
  421.5 96.2 %table_rows.10.dep_ref = f32[1872,1024]{1,0:T(8,128)} custom-call(s32[1]{0:T(128)} %bitcast.12.off_ref, bf16[37984,1024]{1,0:T(8,128)(2,1)} %e_hbm.17, bf16[4096,1024]{1,0:T(8,128)(2,1)} %get-tuple-element.37.x_a, bf16[4096,1024]{1,0:T(8,128)(2,1)} %get-tuple-element.36.x_b, s32[16,1,512]{2,1,0:T(1,128)} %sub.61.lab_ref, f32[16,1,512]{2,1,0:T(1,128)} %div.81.iz_ref, ...), custom_call_target="tpu_custom_call" | custom-call | flops 62813896704 | bytes 16777216 | tf_op jit(solution)/shard_map/table_rows/pallas_call | solution.py:330
  517.9 96.2 %table_rows.11.dep_ref = f32[1872,1024]{1,0:T(8,128)} custom-call(s32[1]{0:T(128)} %bitcast.11.off_ref, bf16[37984,1024]{1,0:T(8,128)(2,1)} %e_hbm.17, bf16[4096,1024]{1,0:T(8,128)(2,1)} %get-tuple-element.37.x_a, bf16[4096,1024]{1,0:T(8,128)(2,1)} %get-tuple-element.36.x_b, s32[16,1,512]{2,1,0:T(1,128)} %sub.61.lab_ref, f32[16,1,512]{2,1,0:T(1,128)} %div.81.iz_ref, ...), custom_call_target="tpu_custom_call" | custom-call | flops 62813896704 | bytes 16777216 | tf_op jit(solution)/shard_map/table_rows/pallas_call | solution.py:330
  614.4 66.8 %table_rows.12.dep_ref = f32[1248,1024]{1,0:T(8,128)} custom-call(s32[1]{0:T(128)} %bitcast.10.off_ref, bf16[37984,1024]{1,0:T(8,128)(2,1)} %e_hbm.17, bf16[4096,1024]{1,0:T(8,128)(2,1)} %get-tuple-element.37.x_a, bf16[4096,1024]{1,0:T(8,128)(2,1)} %get-tuple-element.36.x_b, s32[16,1,512]{2,1,0:T(1,128)} %sub.61.lab_ref, f32[16,1,512]{2,1,0:T(1,128)} %div.81.iz_ref, ...), custom_call_target="tpu_custom_call" | custom-call | flops 41875931136 | bytes 16777216 | tf_op jit(solution)/shard_map/table_rows/pallas_call | solution.py:330
  686.7 38.1 %table_rows.13.dep_ref = f32[624,1024]{1,0:T(8,128)} custom-call(s32[1]{0:T(128)} %bitcast.9.off_ref, bf16[37984,1024]{1,0:T(8,128)(2,1)} %e_hbm.17, bf16[4096,1024]{1,0:T(8,128)(2,1)} %get-tuple-element.37.x_a, bf16[4096,1024]{1,0:T(8,128)(2,1)} %get-tuple-element.36.x_b, s32[16,1,512]{2,1,0:T(1,128)} %sub.61.lab_ref, f32[16,1,512]{2,1,0:T(1,128)} %div.81.iz_ref, ...), custom_call_target="tpu_custom_call" | custom-call | flops 20937965568 | bytes 16777216 | tf_op jit(solution)/shard_map/table_rows/pallas_call | solution.py:330
  724.8 223.5 %grad_x.1 = f32[2048,1024]{1,0:T(8,128)} custom-call(f32[38,1536,1024]{2,1,0:T(8,128)} %get-tuple-element.19.qm_ref, f32[38,512,1024]{2,1,0:T(8,128)} %get-tuple-element.20.qt_ref, bf16[37984,1024]{1,0:T(8,128)(2,1)} %e_hbm.17, f32[2048,1]{1,0:T(8,128)} %copy.28.a_ref, f32[2048,1]{1,0:T(8,128)} %divide_multiply_fusion.b_ref, s32[2048,1]{1,0:T(8,128)} %copy.22.lab_ref, ...), custom_call_target="tpu_custom_call" | custom-call | flops 159316443136 | bytes 311164928 | tf_op jit(solution)/shard_map/grad_x/pallas_call | solution.py:153
  948.4 6.8 slice_select_fusion.1.dep_ref
  955.3 177.5 %table_rows.14.rest_0_ = f32[37984,1024]{1,0:T(8,128)} custom-call(s32[1]{0:T(128)} %constant.21.clone.1.off_ref, bf16[37984,1024]{1,0:T(8,128)(2,1)} %e_hbm.17, bf16[4096,1024]{1,0:T(8,128)(2,1)} %get-tuple-element.37.x_a, bf16[4096,1024]{1,0:T(8,128)(2,1)} %get-tuple-element.36.x_b, s32[16,1,512]{2,1,0:T(1,128)} %sub.61.lab_ref, ...), custom_call_target="tpu_custom_call" | custom-call | flops 119185342464 | bytes 16777216 | tf_op jit(solution)/shard_map/table_rows/pallas_call | solution.py:330
  1132.8 8.6 select_add_fusion.dep_ref
  1142.0 175.4 %table_rows.15.rest_1_ = f32[37984,1024]{1,0:T(8,128)} custom-call(s32[1]{0:T(128)} %constant.22.clone.1.off_ref, bf16[37984,1024]{1,0:T(8,128)(2,1)} %e_hbm.17, bf16[4096,1024]{1,0:T(8,128)(2,1)} %get-tuple-element.37.x_a, bf16[4096,1024]{1,0:T(8,128)(2,1)} %get-tuple-element.36.x_b, s32[16,1,512]{2,1,0:T(1,128)} %sub.61.lab_ref, ...), custom_call_target="tpu_custom_call", output_to_operand_aliasing={{}: (8, {})} | custom-call | flops 119185342464 | bytes 16777216 | tf_op jit(solution)/shard_map/table_rows/pallas_call | solution.py:330
  1317.4 6.9 add.34.dep_ref
  1324.6 176.7 %table_rows.16.rest_1_ = f32[37984,1024]{1,0:T(8,128)} custom-call(s32[1]{0:T(128)} %constant.58.clone.1.off_ref, bf16[37984,1024]{1,0:T(8,128)(2,1)} %e_hbm.17, bf16[4096,1024]{1,0:T(8,128)(2,1)} %get-tuple-element.37.x_a, bf16[4096,1024]{1,0:T(8,128)(2,1)} %get-tuple-element.36.x_b, s32[16,1,512]{2,1,0:T(1,128)} %sub.61.lab_ref, ...), custom_call_target="tpu_custom_call", output_to_operand_aliasing={{}: (9, {})} | custom-call | flops 119185342464 | bytes 16777216 | tf_op jit(solution)/shard_map/table_rows/pallas_call | solution.py:330
  1501.3 9.6 multiply_reduce_fusion
  1510.9 9.0 psum.15
  1519.9 10.2 fusion.5
  1530.1 120.1 %table_rows.17.o_in = f32[37984,1024]{1,0:T(8,128)} custom-call(s32[1]{0:T(128)} %constant.60.clone.1.off_ref, bf16[37984,1024]{1,0:T(8,128)(2,1)} %e_hbm.17, bf16[4096,1024]{1,0:T(8,128)(2,1)} %get-tuple-element.37.x_a, bf16[4096,1024]{1,0:T(8,128)(2,1)} %get-tuple-element.36.x_b, s32[16,1,512]{2,1,0:T(1,128)} %sub.61.lab_ref, ...), custom_call_target="tpu_custom_call", output_to_operand_aliasing={{}: (9, {})} | custom-call | flops 79456894976 | bytes 16777216 | tf_op jit(solution)/shard_map/table_rows/pallas_call | solution.py:330
  1650.3 8.0 place.1
  (77 shorter events, 15.9 us)
Async XLA Ops:
  7.2 281.5 %all-gather.7.cloned.1.call-start = ((), (), s32[]{:S(2)}) async-start(), calls=%async_computation | async-start | bytes 20971520 | tf_op jit(solution)/shard_map/all_gather | solution.py:402
  10.3 4.9 copy-start.6
  10.3 4.9 copy-start.1
  11.0 4.2 copy-start.3
  15.2 3.1 copy-start.10
  18.2 342.5 %all-reduce.2.cloned.1.call-start = ((), (), s32[]{:S(2)}) async-start(), calls=%async_computation.1 | async-start | bytes 262144 | tf_op jit(solution)/shard_map/psum | solution.py:413
  19.6 271.4 %copy-start.8 = (s32[1,2048]{1,0:T(1,128)S(1)}, s32[1,2048]{1,0:T(1,128)}, u32[]{:S(2)}) copy-start(s32[1,2048]{1,0:T(1,128)} %param.9) | copy-start | bytes 24580
  19.6 271.4 %copy-start.11 = (s32[1,2048]{1,0:T(1,128)S(1)}, s32[1,2048]{1,0:T(1,128)}, u32[]{:S(2)}) copy-start(s32[1,2048]{1,0:T(1,128)} %param.8) | copy-start | bytes 24580
  19.6 345.6 %copy-start.4 = (f32[1024]{0:T(1024)S(1)}, f32[1024]{0:T(1024)}, u32[]{:S(2)}) copy-start(f32[1024]{0:T(1024)} %copy-done.3) | copy-start | bytes 12292
  288.6 76.6 %collective-permute-start = (f32[4096,1024]{1,0:T(8,128)}, f32[4096,1024]{1,0:T(8,128)}, u32[]{:S(2)}, u32[]{:S(2)}) collective-permute-start(f32[4096,1024]{1,0:T(8,128)} %all-gather.7.cloned.1.call-done), channel_id=1, source_target_pairs={{0,1},{1,0},{2,3},{3,2},{4,5},{5,4},{6,7},{7,6},{8,9},{9,8},{10,11... | collective-permute-start | bytes 50331656 | tf_op jit(solution)/shard_map/ppermute | solution.py:406
  292.7 0.6 copy-start
  293.3 661.9 %all-gather.9.cloned.1.call-start = ((), (), s32[]{:S(2)}) async-start(), calls=%async_computation.2 | async-start | bytes 12779520 | tf_op jit(solution)/shard_map/all_gather | solution.py:435
  421.3 534.0 %all-gather.11.cloned.1.call-start = ((), (), s32[]{:S(2)}) async-start(), calls=%async_computation.3 | async-start | bytes 38338560 | tf_op jit(solution)/shard_map/all_gather | solution.py:435
  517.8 806.8 %all-gather.13.cloned.1.call-start = ((), (), s32[]{:S(2)}) async-start(), calls=%async_computation.4 | async-start | bytes 38338560 | tf_op jit(solution)/shard_map/all_gather | solution.py:435
  614.1 916.0 %all-gather.17.cloned.1.call-start = ((), (), s32[]{:S(2)}) async-start(), calls=%async_computation.6 | async-start | bytes 25559040 | tf_op jit(solution)/shard_map/all_gather | solution.py:435
  614.4 66.9 %copy-start.9 = (s32[1,2048]{1,0:T(1,128)S(1)}, s32[1,2048]{1,0:T(1,128)}, u32[]{:S(2)}) copy-start(s32[1,2048]{1,0:T(1,128)} %param.9) | copy-start | bytes 24580
  681.2 969.0 %all-gather.15.cloned.1.call-start = ((), (), s32[]{:S(2)}) async-start(), calls=%async_computation.5 | async-start | bytes 12779520 | tf_op jit(solution)/shard_map/all_gather | solution.py:435
  955.2 177.6 %collective-permute-start.1 = (f32[1024,1024]{1,0:T(8,128)}, f32[1024,1024]{1,0:T(8,128)}, u32[]{:S(2)}, u32[]{:S(2)}) collective-permute-start(f32[1024,1024]{1,0:T(8,128)} %slice_select_fusion.1.dep_ref), channel_id=1, source_target_pairs={{0,1},{1,0},{2,3},{3,2},{4,5},{5,4},{6,7},{7,6},{8,9},{9,8},{10,11... | collective-permute-start | bytes 12582920 | tf_op jit(solution)/shard_map/ppermute | solution.py:446
  1141.5 175.9 %collective-permute-start.2 = (f32[1024,1024]{1,0:T(8,128)}, f32[1024,1024]{1,0:T(8,128)}, u32[]{:S(2)}, u32[]{:S(2)}) collective-permute-start(f32[1024,1024]{1,0:T(8,128)} %select_add_fusion.dep_ref), channel_id=1, source_target_pairs={{0,2},{1,3},{2,0},{3,1},{4,6},{5,7},{6,4},{7,5},{8,10},{9,11},{10,... | collective-permute-start | bytes 12582920 | tf_op jit(solution)/shard_map/ppermute | solution.py:446
  1324.3 177.0 %copy-start.2 = (f32[2048]{0:T(1024)S(1)}, f32[2048]{0:T(1024)}, u32[]{:S(2)}) copy-start(f32[2048]{0:T(1024)} %copy-done.1) | copy-start | bytes 24580
  1324.3 177.0 %copy-start.5 = (f32[1024]{0:T(1024)S(1)}, f32[1024]{0:T(1024)}, u32[]{:S(2)}) copy-start(f32[1024]{0:T(1024)} %copy-done.3) | copy-start | bytes 12292
  1324.3 176.9 %collective-permute-start.3 = (f32[1024,1024]{1,0:T(8,128)}, f32[1024,1024]{1,0:T(8,128)}, u32[]{:S(2)}, u32[]{:S(2)}) collective-permute-start(f32[1024,1024]{1,0:T(8,128)} %add.34.dep_ref), channel_id=1, source_target_pairs={{0,1},{1,0},{2,3},{3,2},{4,5},{5,4},{6,7},{7,6},{8,9},{9,8},{10,11... | collective-permute-start | bytes 12582920 | tf_op jit(solution)/shard_map/ppermute | solution.py:446
  1501.3 18.6 %copy-start.7 = (f32[2048]{0:T(1024)S(1)}, f32[2048]{0:T(1024)}, u32[]{:S(2)}) copy-start(f32[2048]{0:T(1024)} %copy-done.6) | copy-start | bytes 24580
Sparse Core Ops, SparseCore 0:
  18.3 156.4 all-gather.6
  293.5 67.2 all-reduce.1
  421.4 97.4 all-gather.8
  520.6 269.3 all-gather.10
  791.7 269.3 all-gather.12
  1062.7 185.0 all-gather.16
  1249.6 98.9 all-gather.14

commit v2 on v1

--- a/solution.py
+++ b/solution.py
@@ -15,10 +15,10 @@
 CFG = dict(
     VB=1024,
     TS=512,
-    RU=624,
+    RU=720,
     CHUNKS=(1, 3, 3, 2, 1),
-    RD=592,
-    CALLS=(6, 6, 6, 4),
+    RD=656,
+    CALLS=(4, 4, 3, 3),
     ABSORB=((0, 1), (), (2,), (3,)),
 )
 ANY = pl.BlockSpec(memory_space=pl.ANY)
@@ -408,9 +408,8 @@
         x_all = tuple((v * gain).astype(jnp.bfloat16) for v in (got, other))
         side = jnp.stack([lab_own, loss_mask.reshape(tokens)]).astype(jnp.float32)
         stats = jnp.stack([jnp.sum(z_sum, axis=-1), jnp.sum(t_lab, axis=-1)])
-        stats = jnp.concatenate([stats, jnp.where(tp == 0, side, 0.0)])
-        stats = lax.dynamic_update_slice(jnp.zeros((n_dp, 4, tokens), jnp.float32), stats[None], (dp, 0, 0))
-        stats = lax.psum(stats, ("dp", "tp"))
+        own = lax.psum(stats, "tp")
+        stats = lax.all_gather(jnp.concatenate([own, side]), "dp", axis=0, tiled=False)
 
         split = stats.reshape(n_dp, 4, 2, half)
         split = jnp.where(core == 0, split, split[:, :, ::-1])
@@ -422,7 +421,6 @@
         shape3 = (n_dp * tokens // ts, 1, ts)
         vecs = ((lab_all - tp * rows).reshape(shape3), (1.0 / z_all).reshape(shape3), scale_all.reshape(shape3))
 
-        own = lax.dynamic_index_in_dim(stats, dp, 0, keepdims=False)
         scale_own = loss_mask.reshape(tokens).astype(jnp.float32) / count
         a_col = (scale_own / own[0])[:, None]
         b_col = (scale_own * (1.0 - own[1] * own[1]))[:, None]

time: 1680 us -> 1510 us (0.90)
  Pallas kernels: 1490 us -> 1350 us
  waiting for transfers between devices: 67.1 us -> 0.19 us
  blocking collectives: 8.97 us -> 49.2 us
    pallas_call x9, Pallas kernels: 985 us -> 846 us  [table_rows(): pl.pallas_call(kernel, grid=(nblk,), in_specs=[pl.BlockSpec(memory_space=...]
    psum x1 -> x0, waiting for transfers between devices: 66.9 us -> none  [local_step(): stats = lax.psum(stats, ('dp', 'tp'))]
    psum x0 -> x1, blocking collectives: none -> 29.8 us  [local_step(): own = lax.psum(stats, 'tp')]
  transfers between devices with their start and end apart: 11 -> 10, of which waited for: 1 -> 0; matrix products, arithmetic and copies ran while one was open for 3% -> 3% of each run, Pallas kernels for 86% -> 87%
where the time goes in v2:
time: 1510 us; the launch traced here: 1500 us
  Pallas kernels  1350 us (89%)
  other arithmetic  74.8 us (5%)
  blocking collectives  49.2 us (3%)
  between operations  17.3 us (1%)
    pallas_call x9, Pallas kernels, table_rows(): pl.pallas_call(kernel, grid=(nblk,), in_specs=[pl.BlockSpec(memory_space=...  846 us
    pallas_call x1, Pallas kernels, first_pass(): pl.pallas_call(kernel, grid=(n + 1,), in_specs=[pl.BlockSpec((tokens, dim...  269 us
    pallas_call x1, Pallas kernels, grad_x(): pl.pallas_call(kernel, grid=(n,), in_specs=[pl.BlockSpec((1, tokens - ts,...  224 us
  transfers between devices with their start and end apart: 10, of which 0 were waited for; matrix products, arithmetic and copies ran while one was open for 3% of the time, Pallas kernels for 87%

profile of v2, /device:TPU:0, one launch (start us, length us, event | category | flops | bytes accessed | tf_op | source)
XLA Modules:
  0.0 1498.0 jit_solution(16047296793317234198)
XLA Ops:
  7.2 3.1 fusion.3
  11.0 4.2 fusion.1
  15.2 3.0 slice_select_fusion
  19.7 269.0 %first_pass.1 = (f32[38,1536,1024]{2,1,0:T(8,128)}, f32[38,512,1024]{2,1,0:T(8,128)}, f32[2048,128]{1,0:T(8,128)}, f32[2048,128]{1,0:T(8,128)}) custom-call(bf16[2048,1024]{1,0:T(8,128)(2,1)} %get-tuple-element.33.x_ref.dep_ref, s32[2048,1]{1,0:T(8,128)} %copy.21.lab_ref, bf16[37984,1024]{1,0:T(8,128)(2,1)} %e_hbm.17), custom_call_target="tpu_custom_call" | custom-call | flops 159316443136 | bytes 311164928 | tf_op jit(solution)/shard_map/first_pass/pallas_call | solution.py:94
  292.7 29.8 %psum.14 = f32[2,2048]{1,0:T(2,128)S(1)} all-reduce(f32[2,2048]{1,0:T(2,128)S(1)} %pad_maximum_fusion), channel_id=1, replica_groups=mesh['dp'=4,'tp'=4] {'tp'}, use_global_device_ids=true, to_apply=%region_3.4 | all-reduce | flops 4096 | bytes 32768 | tf_op jit(solution)/shard_map/psum | solution.py:411
  323.1 9.2 all-gather.1
  335.8 18.2 %multiply_convert_fusion = (bf16[4096,1024]{1,0:T(8,128)(2,1)}, bf16[4096,1024]{1,0:T(8,128)(2,1)}) fusion(f32[4096,1024]{1,0:T(8,128)} %collective-permute-done, f32[1024]{0:T(1024)S(1)} %copy-done.5, f32[4096,1024]{1,0:T(8,128)} %all-gather.9.cloned.1.call-done), kind=kLoop, calls=%fused_computation | loop fusion | flops 16777216 | bytes 50335744 | tf_op jit(solution)/shard_map/convert_element_type | solution.py:408
  354.0 42.1 %table_rows.9.dep_ref = f32[720,1024]{1,0:T(8,128)} custom-call(s32[1]{0:T(128)} %bitcast.12.off_ref, bf16[37984,1024]{1,0:T(8,128)(2,1)} %e_hbm.17, bf16[4096,1024]{1,0:T(8,128)(2,1)} %get-tuple-element.39.x_a, bf16[4096,1024]{1,0:T(8,128)(2,1)} %get-tuple-element.38.x_b, s32[16,1,512]{2,1,0:T(1,128)} %sub.58.lab_ref, f32[16,1,512]{2,1,0:T(1,128)} %div.83.iz_ref, ...), custom_call_target="tpu_custom_call" | custom-call | flops 24159191040 | bytes 16777216 | tf_op jit(solution)/shard_map/table_rows/pallas_call | solution.py:330
  396.4 109.1 %table_rows.10.dep_ref = f32[2160,1024]{1,0:T(8,128)} custom-call(s32[1]{0:T(128)} %bitcast.11.off_ref, bf16[37984,1024]{1,0:T(8,128)(2,1)} %e_hbm.17, bf16[4096,1024]{1,0:T(8,128)(2,1)} %get-tuple-element.39.x_a, bf16[4096,1024]{1,0:T(8,128)(2,1)} %get-tuple-element.38.x_b, s32[16,1,512]{2,1,0:T(1,128)} %sub.58.lab_ref, f32[16,1,512]{2,1,0:T(1,128)} %div.83.iz_ref, ...), custom_call_target="tpu_custom_call" | custom-call | flops 72477573120 | bytes 16777216 | tf_op jit(solution)/shard_map/table_rows/pallas_call | solution.py:330
  505.8 109.1 %table_rows.11.dep_ref = f32[2160,1024]{1,0:T(8,128)} custom-call(s32[1]{0:T(128)} %bitcast.10.off_ref, bf16[37984,1024]{1,0:T(8,128)(2,1)} %e_hbm.17, bf16[4096,1024]{1,0:T(8,128)(2,1)} %get-tuple-element.39.x_a, bf16[4096,1024]{1,0:T(8,128)(2,1)} %get-tuple-element.38.x_b, s32[16,1,512]{2,1,0:T(1,128)} %sub.58.lab_ref, f32[16,1,512]{2,1,0:T(1,128)} %div.83.iz_ref, ...), custom_call_target="tpu_custom_call" | custom-call | flops 72477573120 | bytes 16777216 | tf_op jit(solution)/shard_map/table_rows/pallas_call | solution.py:330
  615.2 75.5 %table_rows.12.dep_ref = f32[1440,1024]{1,0:T(8,128)} custom-call(s32[1]{0:T(128)} %bitcast.9.off_ref, bf16[37984,1024]{1,0:T(8,128)(2,1)} %e_hbm.17, bf16[4096,1024]{1,0:T(8,128)(2,1)} %get-tuple-element.39.x_a, bf16[4096,1024]{1,0:T(8,128)(2,1)} %get-tuple-element.38.x_b, s32[16,1,512]{2,1,0:T(1,128)} %sub.58.lab_ref, f32[16,1,512]{2,1,0:T(1,128)} %div.83.iz_ref, ...), custom_call_target="tpu_custom_call" | custom-call | flops 48318382080 | bytes 16777216 | tf_op jit(solution)/shard_map/table_rows/pallas_call | solution.py:330
  694.2 42.6 %table_rows.13.dep_ref = f32[720,1024]{1,0:T(8,128)} custom-call(s32[1]{0:T(128)} %bitcast.8.off_ref, bf16[37984,1024]{1,0:T(8,128)(2,1)} %e_hbm.17, bf16[4096,1024]{1,0:T(8,128)(2,1)} %get-tuple-element.39.x_a, bf16[4096,1024]{1,0:T(8,128)(2,1)} %get-tuple-element.38.x_b, s32[16,1,512]{2,1,0:T(1,128)} %sub.58.lab_ref, f32[16,1,512]{2,1,0:T(1,128)} %div.83.iz_ref, ...), custom_call_target="tpu_custom_call" | custom-call | flops 24159191040 | bytes 16777216 | tf_op jit(solution)/shard_map/table_rows/pallas_call | solution.py:330
  736.7 223.5 %grad_x.1 = f32[2048,1024]{1,0:T(8,128)} custom-call(f32[38,1536,1024]{2,1,0:T(8,128)} %get-tuple-element.19.qm_ref, f32[38,512,1024]{2,1,0:T(8,128)} %get-tuple-element.20.qt_ref, bf16[37984,1024]{1,0:T(8,128)(2,1)} %e_hbm.17, f32[2048,1]{1,0:T(8,128)} %copy.24.a_ref, f32[2048,1]{1,0:T(8,128)} %copy.25.b_ref, s32[2048,1]{1,0:T(8,128)} %copy.21.lab_ref, ...), custom_call_target="tpu_custom_call" | custom-call | flops 159316443136 | bytes 311164928 | tf_op jit(solution)/shard_map/grad_x/pallas_call | solution.py:153
  960.3 6.8 slice_select_fusion.1.dep_ref
  967.2 133.2 %table_rows.14.rest_0_ = f32[37984,1024]{1,0:T(8,128)} custom-call(s32[1]{0:T(128)} %constant.21.clone.1.off_ref, bf16[37984,1024]{1,0:T(8,128)(2,1)} %e_hbm.17, bf16[4096,1024]{1,0:T(8,128)(2,1)} %get-tuple-element.39.x_a, bf16[4096,1024]{1,0:T(8,128)(2,1)} %get-tuple-element.38.x_b, s32[16,1,512]{2,1,0:T(1,128)} %sub.58.lab_ref, ...), custom_call_target="tpu_custom_call" | custom-call | flops 88046829568 | bytes 16777216 | tf_op jit(solution)/shard_map/table_rows/pallas_call | solution.py:330
  1100.4 8.6 select_add_fusion.dep_ref
  1109.4 131.8 %table_rows.15.rest_1_ = f32[37984,1024]{1,0:T(8,128)} custom-call(s32[1]{0:T(128)} %constant.50.clone.1.off_ref, bf16[37984,1024]{1,0:T(8,128)(2,1)} %e_hbm.17, bf16[4096,1024]{1,0:T(8,128)(2,1)} %get-tuple-element.39.x_a, bf16[4096,1024]{1,0:T(8,128)(2,1)} %get-tuple-element.38.x_b, s32[16,1,512]{2,1,0:T(1,128)} %sub.58.lab_ref, ...), custom_call_target="tpu_custom_call", output_to_operand_aliasing={{}: (8, {})} | custom-call | flops 88046829568 | bytes 16777216 | tf_op jit(solution)/shard_map/table_rows/pallas_call | solution.py:330
  1241.2 6.9 add.28.dep_ref
  1248.4 101.8 %table_rows.16.rest_1_ = f32[37984,1024]{1,0:T(8,128)} custom-call(s32[1]{0:T(128)} %constant.51.clone.1.off_ref, bf16[37984,1024]{1,0:T(8,128)(2,1)} %e_hbm.17, bf16[4096,1024]{1,0:T(8,128)(2,1)} %get-tuple-element.39.x_a, bf16[4096,1024]{1,0:T(8,128)(2,1)} %get-tuple-element.38.x_b, s32[16,1,512]{2,1,0:T(1,128)} %sub.58.lab_ref, ...), custom_call_target="tpu_custom_call", output_to_operand_aliasing={{}: (9, {})} | custom-call | flops 66035122176 | bytes 16777216 | tf_op jit(solution)/shard_map/table_rows/pallas_call | solution.py:330
  1350.2 9.2 multiply_reduce_fusion
  1359.4 10.2 psum.15
  1369.6 10.2 fusion.5
  1379.8 101.2 %table_rows.17.o_in = f32[37984,1024]{1,0:T(8,128)} custom-call(s32[1]{0:T(128)} %constant.53.clone.1.off_ref, bf16[37984,1024]{1,0:T(8,128)(2,1)} %e_hbm.17, bf16[4096,1024]{1,0:T(8,128)(2,1)} %get-tuple-element.39.x_a, bf16[4096,1024]{1,0:T(8,128)(2,1)} %get-tuple-element.38.x_b, s32[16,1,512]{2,1,0:T(1,128)} %sub.58.lab_ref, ...), custom_call_target="tpu_custom_call", output_to_operand_aliasing={{}: (9, {})} | custom-call | flops 66035122176 | bytes 16777216 | tf_op jit(solution)/shard_map/table_rows/pallas_call | solution.py:330
  1481.0 8.5 place.1
  (74 shorter events, 13.9 us)
Async XLA Ops:
  7.2 281.5 %all-gather.9.cloned.1.call-start = ((), (), s32[]{:S(2)}) async-start(), calls=%async_computation | async-start | bytes 20971520 | tf_op jit(solution)/shard_map/all_gather | solution.py:402
  10.3 4.9 copy-start.7
  10.3 4.9 copy-start.2
  11.0 4.2 copy-start.4
  15.2 3.1 copy-start.9
  18.2 949.0 %all-gather.11.cloned.1.call-start = ((), (), s32[]{:S(2)}) async-start(), calls=%async_computation.1 | async-start | bytes 14745600 | tf_op jit(solution)/shard_map/all_gather | solution.py:433
  19.7 271.4 %copy-start.10 = (s32[1,2048]{1,0:T(1,128)S(1)}, s32[1,2048]{1,0:T(1,128)}, u32[]{:S(2)}) copy-start(s32[1,2048]{1,0:T(1,128)} %param.8) | copy-start | bytes 24580
  19.7 271.4 %copy-start.11 = (s32[1,2048]{1,0:T(1,128)S(1)}, s32[1,2048]{1,0:T(1,128)}, u32[]{:S(2)}) copy-start(s32[1,2048]{1,0:T(1,128)} %param.9) | copy-start | bytes 24580
  19.7 316.1 %copy-start.5 = (f32[1024]{0:T(1024)S(1)}, f32[1024]{0:T(1024)}, u32[]{:S(2)}) copy-start(f32[1024]{0:T(1024)} %copy-done.4) | copy-start | bytes 12292
  288.7 47.1 %collective-permute-start = (f32[4096,1024]{1,0:T(8,128)}, f32[4096,1024]{1,0:T(8,128)}, u32[]{:S(2)}, u32[]{:S(2)}) collective-permute-start(f32[4096,1024]{1,0:T(8,128)} %all-gather.9.cloned.1.call-done), channel_id=1, source_target_pairs={{0,1},{1,0},{2,3},{3,2},{4,5},{5,4},{6,7},{7,6},{8,9},{9,8},{10,11... | collective-permute-start | bytes 50331656 | tf_op jit(solution)/shard_map/ppermute | solution.py:406
  322.4 0.6 copy-start
  396.1 571.0 %all-gather.13.cloned.1.call-start = ((), (), s32[]{:S(2)}) async-start(), calls=%async_computation.2 | async-start | bytes 44236800 | tf_op jit(solution)/shard_map/all_gather | solution.py:433
  505.5 742.9 %all-gather.15.cloned.1.call-start = ((), (), s32[]{:S(2)}) async-start(), calls=%async_computation.3 | async-start | bytes 44236800 | tf_op jit(solution)/shard_map/all_gather | solution.py:433
  614.9 764.9 %all-gather.19.cloned.1.call-start = ((), (), s32[]{:S(2)}) async-start(), calls=%async_computation.5 | async-start | bytes 29491200 | tf_op jit(solution)/shard_map/all_gather | solution.py:433
  615.2 75.6 %copy-start.1 = (f32[2,2048]{1,0:T(2,128)S(1)}, f32[2,2048]{1,0:T(2,128)}, u32[]{:S(2)}) copy-start(f32[2,2048]{1,0:T(2,128)} %copy-done) | copy-start | bytes 49156
  615.2 75.6 %copy-start.12 = (s32[1,2048]{1,0:T(1,128)S(1)}, s32[1,2048]{1,0:T(1,128)}, u32[]{:S(2)}) copy-start(s32[1,2048]{1,0:T(1,128)} %param.9) | copy-start | bytes 24580
  690.8 790.2 %all-gather.17.cloned.1.call-start = ((), (), s32[]{:S(2)}) async-start(), calls=%async_computation.4 | async-start | bytes 14745600 | tf_op jit(solution)/shard_map/all_gather | solution.py:433
  967.1 133.3 %collective-permute-start.1 = (f32[1024,1024]{1,0:T(8,128)}, f32[1024,1024]{1,0:T(8,128)}, u32[]{:S(2)}, u32[]{:S(2)}) collective-permute-start(f32[1024,1024]{1,0:T(8,128)} %slice_select_fusion.1.dep_ref), channel_id=1, source_target_pairs={{0,1},{1,0},{2,3},{3,2},{4,5},{5,4},{6,7},{7,6},{8,9},{9,8},{10,11... | collective-permute-start | bytes 12582920 | tf_op jit(solution)/shard_map/ppermute | solution.py:444
  1109.0 132.2 %collective-permute-start.2 = (f32[1024,1024]{1,0:T(8,128)}, f32[1024,1024]{1,0:T(8,128)}, u32[]{:S(2)}, u32[]{:S(2)}) collective-permute-start(f32[1024,1024]{1,0:T(8,128)} %select_add_fusion.dep_ref), channel_id=1, source_target_pairs={{0,2},{1,3},{2,0},{3,1},{4,6},{5,7},{6,4},{7,5},{8,10},{9,11},{10,... | collective-permute-start | bytes 12582920 | tf_op jit(solution)/shard_map/ppermute | solution.py:444
  1248.2 102.0 %copy-start.3 = (f32[2048]{0:T(1024)S(1)}, f32[2048]{0:T(1024)}, u32[]{:S(2)}) copy-start(f32[2048]{0:T(1024)} %copy-done.2) | copy-start | bytes 24580
  1248.2 102.0 %copy-start.6 = (f32[1024]{0:T(1024)S(1)}, f32[1024]{0:T(1024)}, u32[]{:S(2)}) copy-start(f32[1024]{0:T(1024)} %copy-done.4) | copy-start | bytes 12292
  1248.2 102.0 %collective-permute-start.3 = (f32[1024,1024]{1,0:T(8,128)}, f32[1024,1024]{1,0:T(8,128)}, u32[]{:S(2)}, u32[]{:S(2)}) collective-permute-start(f32[1024,1024]{1,0:T(8,128)} %add.28.dep_ref), channel_id=1, source_target_pairs={{0,1},{1,0},{2,3},{3,2},{4,5},{5,4},{6,7},{7,6},{8,9},{9,8},{10,11... | collective-permute-start | bytes 12582920 | tf_op jit(solution)/shard_map/ppermute | solution.py:444
  1350.2 19.4 %copy-start.8 = (f32[2048]{0:T(1024)S(1)}, f32[2048]{0:T(1024)}, u32[]{:S(2)}) copy-start(f32[2048]{0:T(1024)} %copy-done.7) | copy-start | bytes 24580
Sparse Core Ops, SparseCore 0:
  18.3 156.4 all-gather.8
  396.3 111.1 all-gather.10
  509.3 309.7 all-gather.12
  820.8 309.7 all-gather.14
  1132.2 210.9 all-gather.18
  1344.9 112.1 all-gather.16
